TPU v7x, 32 devices: a whole 2x2x4 slice. The times are simulated.
32 devices in a mesh: grp: 4 (over x, core), mem: 8 (over z, y).
Axes of the slice: x: 2, y: 2, z: 4, core: 2. Of those that a mesh axis runs over, the one named last changes fastest.
Arguments:
- layer_input: bfloat16 [65536, 128], P(('grp', 'mem')), may hold values from -6 to 6
- history: bfloat16 [65536, 128], P(('grp', 'mem')), may hold values from -6 to 6
- adjacency: bfloat16 [4, 8, 16, 8, 128, 128], P('grp', 'mem'), may hold values from 0 to 0.049804688
- tile_source: int32 [4, 8, 16, 8], P('grp', 'mem'), may hold values from 0 to 31, as said below
- counts: int32 [4, 8, 16], P('grp', 'mem'), may hold values from 1 to 8, as said below
- requests: int32 [4, 8, 8, 1], P('grp', 'mem'), may hold values from 0 to 15
- send_ids: int32 [4, 8, 4, 2], P('grp', 'mem'), may hold values from 0 to 15
- weight: bfloat16 [128, 128], replicated, may hold values from -0.5 to 0.5
- layer_bias: float32 [128], replicated, may hold values from -3 to 3
- cotangent: bfloat16 [65536, 128], P(('grp', 'mem')), may hold values from -6 to 6
Outputs:
- layer_output: bfloat16 [65536, 128], P(('grp', 'mem'))
- input_grad: bfloat16 [65536, 128], P(('grp', 'mem'))
- weight_grad: float32 [128, 128], replicated
- bias_grad: float32 [128], replicated
Inputs may be any that keep to these rules, and one draw needn't show every extreme that they name: `tile_source`: index into the partition's source table; every source block from 16 onward is named by at least one live slot of the partition. `counts`: slots at or past a row block's count are padding, whatever their tiles hold; a partition's live slots together number at least 16. `requests`: block numbers within the asked partition; repeats may occur. `send_ids`: block numbers within the sending partition; repeats may occur.
All inputs are finite; a program needn't handle non-finite values.
Results may differ from a plain program's by a relative error of at most 0.007.
Values may be sent and summed in bfloat16 or wider, within the bound.
A program may use at most 64 MiB of HBM per device.

v0:
```python
import functools
import math

import jax
import jax.numpy as jnp
from jax import lax
from jax.experimental import pallas as pl
from jax.experimental.pallas import tpu as pltpu
from jax.sharding import PartitionSpec as P

F32 = jnp.float32
BF16 = jnp.bfloat16
MESH = pl.DeviceIdType.MESH
GELU_C = math.sqrt(2.0 / math.pi)
GELU_A = 0.044715
ROW_UNROLL = 4
TILE_UNROLL = 4


def dot(a, b, contract):
    return lax.dot_general(a, b, (contract, ((), ())), preferred_element_type=F32)


def layer_kernel(
    dims,
    tile_source,
    counts,
    requests,
    send_ids,
    x_hbm,
    hist_hbm,
    adj_hbm,
    cot_hbm,
    weight,
    bias,
    out_ref,
    grad_ref,
    wsum_ref,
    bsum_ref,
    table,
    hist,
    adj,
    cot,
    outbox,
    inbox,
    served,
    outgoing,
    grad_t,
    running,
    sort_vmem,
    sort_smem,
    parts,
    scattered,
    gathered,
    result,
    local_sem,
    req_send,
    req_recv,
    fetch_send,
    fetch_recv,
    border_send,
    border_recv,
    a_send,
    a_recv,
    b_send,
    b_recv,
    c_send,
    c_recv,
):
    groups, members, rows, slots, per_group, scale = dims
    tiles = rows * slots
    g_me = lax.axis_index("grp")
    m_me = lax.axis_index("mem")
    block = hist.shape[1]
    feats = hist.shape[2]
    zero_block = table.shape[0] - 1
    border_at = rows + members

    def mem_peer(step):
        return lax.rem(m_me + step, members)

    def grp_peer(step):
        return lax.rem(g_me + step, groups)

    hist_copy = pltpu.make_async_copy(hist_hbm, hist, local_sem.at[0])
    adj_copy = pltpu.make_async_copy(adj_hbm, adj, local_sem.at[1])
    x_copy = pltpu.make_async_copy(x_hbm, table.at[pl.ds(0, rows)], local_sem.at[2])
    cot_copy = pltpu.make_async_copy(cot_hbm, cot, local_sem.at[3])
    hist_copy.start()
    barrier = pltpu.get_barrier_semaphore()
    for step in range(1, members):
        pl.semaphore_signal(barrier, inc=1, device_id={"mem": mem_peer(step)}, device_id_type=MESH)
    for step in range(1, groups):
        pl.semaphore_signal(barrier, inc=1, device_id={"grp": grp_peer(step)}, device_id_type=MESH)
    x_copy.start()
    adj_copy.start()
    cot_copy.start()

    for m in range(members):
        outbox[m] = jnp.full(outbox.shape[1:], requests[0, 0, 0, m], jnp.int32)
    table[zero_block] = jnp.zeros((block, feats), BF16)
    hist_copy.wait()
    for g in range(groups):
        for b in range(per_group):
            outgoing[g, b] = hist[send_ids[0, 0, b, g]]
    pl.semaphore_wait(barrier, members + groups - 2)

    def req_copy(slot_there, peer):
        return pltpu.make_async_remote_copy(
            src_ref=outbox.at[peer],
            dst_ref=inbox.at[slot_there],
            send_sem=req_send.at[peer],
            recv_sem=req_recv.at[slot_there],
            device_id={"mem": peer},
            device_id_type=MESH,
        )

    def fetch_copy(slot_there, peer):
        return pltpu.make_async_remote_copy(
            src_ref=served.at[peer],
            dst_ref=table.at[rows + slot_there],
            send_sem=fetch_send.at[peer],
            recv_sem=fetch_recv.at[slot_there],
            device_id={"mem": peer},
            device_id_type=MESH,
        )

    def border_copy(slot_there, peer):
        return pltpu.make_async_remote_copy(
            src_ref=outgoing.at[peer],
            dst_ref=table.at[pl.ds(border_at + slot_there * per_group, per_group)],
            send_sem=border_send.at[peer],
            recv_sem=border_recv.at[slot_there],
            device_id={"grp": peer},
            device_id_type=MESH,
        )

    for step in range(1, members):
        req_copy(m_me, mem_peer(step)).start()
    for step in range(1, groups):
        border_copy(g_me, grp_peer(step)).start()

    table[rows + m_me] = hist[requests[0, 0, 0, m_me]]
    for b in range(per_group):
        table[border_at + g_me * per_group + b] = hist[send_ids[0, 0, b, g_me]]

    for step in range(1, members):
        peer = mem_peer(step)
        req_copy(peer, peer).wait_recv()
        wanted = inbox[peer][0, 0]
        served[peer] = hist[wanted]
        fetch_copy(m_me, peer).start()

    lane = lax.broadcasted_iota(jnp.int32, (1, tiles), 1)

    def key_row(r, keys):
        live = counts[0, 0, r]
        for k in range(slots):
            source = tile_source[0, 0, k, r]
            target = jnp.where((k < live) & (source < rows), source, rows)
            at = r * slots + k
            keys = jnp.where(lane == at, target * tiles + at, keys)
        return keys

    keys = lax.fori_loop(0, rows, key_row, jnp.zeros((1, tiles), jnp.int32))
    across = jnp.broadcast_to(keys, (tiles, tiles))
    down = across.T
    place = lax.broadcasted_iota(jnp.int32, (tiles, tiles), 1)

    def count(where, axis):
        return jnp.sum(jnp.where(where, 1, 0), axis=axis, keepdims=True)

    rank = count(across < down, 1)
    first = count(across < (down // tiles) * tiles, 1)
    placed = rank == place
    below = count(down < place * tiles, 0)
    upto = count(down < (place + 1) * tiles, 0)
    sort_vmem[0:1, :] = jnp.sum(jnp.where(placed, down, 0), axis=0, keepdims=True)
    sort_vmem[1:2, :] = jnp.where(upto > below, upto, 0)
    sort_vmem[2:3, :] = count(placed & (rank > first), 0)
    sort_copy = pltpu.make_async_copy(sort_vmem, sort_smem, local_sem.at[4])
    sort_copy.start()
    running[0] = jnp.zeros((feats, block), F32)

    x_copy.wait()
    adj_copy.wait()
    cot_copy.wait()
    sort_copy.wait()
    for step in range(1, groups):
        peer = grp_peer(step)
        border_copy(peer, peer).wait_recv()
    for step in range(1, members):
        peer = mem_peer(step)
        fetch_copy(peer, peer).wait_recv()

    def forward(r, live):
        sources = []
        for k in range(slots):
            at = jnp.where(k < live, tile_source[0, 0, k, r], zero_block)
            sources.append(table[at])
        wide = jnp.concatenate([adj[r, k] for k in range(slots)], axis=1)
        tall = jnp.concatenate(sources, axis=0)
        agg = dot(wide, tall, ((1,), (0,))).astype(BF16)
        pre = dot(agg, weight[...], ((1,), (0,))) + bias[...]
        square = pre * pre
        t = jnp.tanh(GELU_C * (pre + GELU_A * (square * pre)))
        half = 0.5 * (1.0 + t)
        out_ref[r] = (pre * half).astype(BF16)
        slope = half + (0.5 * pre) * (1.0 - t * t) * (GELU_C * (1.0 + (3.0 * GELU_A) * square))
        grad_pre = (cot[r].astype(F32) * slope).astype(BF16)
        grad_t[r] = dot(weight[...], grad_pre, ((1,), (1,))).astype(BF16)
        return (
            dot(agg, grad_pre, ((0,), (0,))),
            jnp.sum(grad_pre.astype(F32), axis=0, keepdims=True),
        )

    def forward_rows(i, carry):
        w_sum, b_sum = carry
        for u in range(ROW_UNROLL):
            r = i * ROW_UNROLL + u
            w_part, b_part = forward(r, counts[0, 0, r])
            w_sum = w_sum + w_part
            b_sum = b_sum + b_part
        return w_sum, b_sum

    w_sum, b_sum = lax.fori_loop(
        0,
        rows // ROW_UNROLL,
        forward_rows,
        (jnp.zeros((feats, feats), F32), jnp.zeros((1, feats), F32)),
    )

    share = feats // groups
    for g in range(groups):
        parts[g, 0:share] = w_sum[g * share : (g + 1) * share]
        parts[g, share : share + 8] = jnp.broadcast_to(b_sum, (8, feats))

    def a_copy(slot_there, peer):
        return pltpu.make_async_remote_copy(
            src_ref=parts.at[peer],
            dst_ref=scattered.at[slot_there],
            send_sem=a_send.at[peer],
            recv_sem=a_recv.at[slot_there],
            device_id={"grp": peer},
            device_id_type=MESH,
        )

    def b_copy(slot_there, peer):
        return pltpu.make_async_remote_copy(
            src_ref=gathered.at[m_me],
            dst_ref=gathered.at[slot_there],
            send_sem=b_send.at[peer],
            recv_sem=b_recv.at[slot_there],
            device_id={"mem": peer},
            device_id_type=MESH,
        )

    def c_copy(slot_there, peer):
        return pltpu.make_async_remote_copy(
            src_ref=result.at[g_me],
            dst_ref=result.at[slot_there],
            send_sem=c_send.at[peer],
            recv_sem=c_recv.at[slot_there],
            device_id={"grp": peer},
            device_id_type=MESH,
        )

    for step in range(1, groups):
        a_copy(g_me, grp_peer(step)).start()
    scattered[g_me] = parts[g_me]

    def backward_tiles(i, carry):
        for u in range(TILE_UNROLL):
            p = i * TILE_UNROLL + u
            key = sort_smem[0, p]
            j = key % tiles
            term = dot(grad_t[j // slots], adj[j // slots, j % slots], ((1,), (0,)))
            running[p + 1] = term + jnp.where(sort_smem[2, p] > 0, running[p], 0.0)
        return carry

    trips = tiles // TILE_UNROLL
    carry = lax.fori_loop(0, trips // 2, backward_tiles, jnp.int32(0))

    for step in range(1, groups):
        peer = grp_peer(step)
        a_copy(peer, peer).wait_recv()
    chunk = scattered[0]
    for g in range(1, groups):
        chunk = chunk + scattered[g]
    gathered[m_me] = chunk
    for step in range(1, members):
        b_copy(m_me, mem_peer(step)).start()

    carry = lax.fori_loop(trips // 2, trips, backward_tiles, carry)
    for c in range(rows):
        grad_ref[c] = running[sort_smem[1, c]].T.astype(BF16)

    for step in range(1, members):
        peer = mem_peer(step)
        b_copy(peer, peer).wait_recv()
    chunk = gathered[0]
    for m in range(1, members):
        chunk = chunk + gathered[m]
    result[g_me] = chunk * scale
    for step in range(1, groups):
        c_copy(g_me, grp_peer(step)).start()

    for step in range(1, members):
        peer = mem_peer(step)
        req_copy(m_me, peer).wait_send()
        fetch_copy(m_me, peer).wait_send()
        b_copy(m_me, peer).wait_send()
    for step in range(1, groups):
        peer = grp_peer(step)
        border_copy(g_me, peer).wait_send()
        a_copy(g_me, peer).wait_send()
        c_copy(g_me, peer).wait_send()
    for step in range(1, groups):
        peer = grp_peer(step)
        c_copy(peer, peer).wait_recv()
    for g in range(groups):
        wsum_ref[g * share : (g + 1) * share] = result[g, 0:share]
    bsum_ref[...] = result[0, share : share + 1]


def per_device(
    layer_input,
    history,
    adjacency,
    tile_source,
    counts,
    requests,
    send_ids,
    weight,
    layer_bias,
    cotangent,
):
    rows, slots, block = adjacency.shape[2:5]
    feats = layer_input.shape[1]
    members = lax.axis_size("mem")
    groups = lax.axis_size("grp")
    per_group = send_ids.shape[3]
    assert requests.shape[3] == 1
    tiles = rows * slots
    scale = (layer_input.shape[0] * groups * members) ** (-0.5)
    share = feats // groups + 8
    sources = rows + members + groups * per_group + 1
    blocked = (rows, block, feats)
    dma = pltpu.SemaphoreType.DMA
    smem = pl.BlockSpec(memory_space=pltpu.SMEM)
    vmem = pl.BlockSpec(memory_space=pltpu.VMEM)
    hbm = pl.BlockSpec(memory_space=pltpu.HBM)
    out, grad, w_sum, b_sum = pl.pallas_call(
        functools.partial(layer_kernel, (groups, members, rows, slots, per_group, scale)),
        out_shape=(
            jax.ShapeDtypeStruct(blocked, BF16),
            jax.ShapeDtypeStruct(blocked, BF16),
            jax.ShapeDtypeStruct((feats, feats), F32),
            jax.ShapeDtypeStruct((1, feats), F32),
        ),
        in_specs=[smem] * 4 + [hbm] * 4 + [vmem] * 2,
        out_specs=(vmem,) * 4,
        scratch_shapes=[
            pltpu.VMEM((sources, block, feats), BF16),
            pltpu.VMEM(blocked, BF16),
            pltpu.VMEM((rows, slots, block, block), BF16),
            pltpu.VMEM(blocked, BF16),
            pltpu.VMEM((members, 8, 128), jnp.int32),
            pltpu.VMEM((members, 8, 128), jnp.int32),
            pltpu.VMEM((members, block, feats), BF16),
            pltpu.VMEM((groups, per_group, block, feats), BF16),
            pltpu.VMEM((rows, feats, block), BF16),
            pltpu.VMEM((tiles + 1, feats, block), F32),
            pltpu.VMEM((8, tiles), jnp.int32),
            pltpu.SMEM((8, tiles), jnp.int32),
            pltpu.VMEM((groups, share, feats), F32),
            pltpu.VMEM((groups, share, feats), F32),
            pltpu.VMEM((members, share, feats), F32),
            pltpu.VMEM((groups, share, feats), F32),
            dma((5,)),
            dma((members,)),
            dma((members,)),
            dma((members,)),
            dma((members,)),
            dma((groups,)),
            dma((groups,)),
            dma((groups,)),
            dma((groups,)),
            dma((members,)),
            dma((members,)),
            dma((groups,)),
            dma((groups,)),
        ],
        compiler_params=pltpu.CompilerParams(
            collective_id=0, has_side_effects=True, vmem_limit_bytes=67043328
        ),
        name="gcn_layer",
    )(
        jnp.swapaxes(tile_source, 2, 3),
        counts,
        jnp.swapaxes(requests, 2, 3),
        jnp.swapaxes(send_ids, 2, 3),
        layer_input.reshape(blocked),
        history.reshape(blocked),
        adjacency.reshape(rows, slots, block, block),
        cotangent.reshape(blocked),
        weight,
        layer_bias.reshape(1, feats),
    )
    return (
        out.reshape(-1, feats),
        grad.reshape(-1, feats),
        w_sum,
        b_sum.reshape(feats),
    )


def solution(mesh):
    return jax.shard_map(
        per_device,
        mesh=mesh,
        in_specs=(
            P(("grp", "mem"), None),
            P(("grp", "mem"), None),
            P("grp", "mem", None, None, None, None),
            P("grp", "mem", None, None),
            P("grp", "mem", None),
            P("grp", "mem", None, None),
            P("grp", "mem", None, None),
            P(),
            P(),
            P(("grp", "mem"), None),
        ),
        out_specs=(P(("grp", "mem"), None), P(("grp", "mem"), None), P(), P()),
        check_vma=False,
    )
```

profile of v0, /device:TPU:0, one launch (start us, length us, event | category | flops | bytes accessed | tf_op | source)
XLA Modules:
  0.0 42.2 jit_solution(5896741954367433438)
XLA Ops:
  0.6 35.2 %gcn_layer.1 = (bf16[16,128,128]{2,1,0:T(8,128)(2,1)}, bf16[16,128,128]{2,1,0:T(8,128)(2,1)}, f32[128,128]{1,0:T(8,128)}, f32[1,128]{1,0:T(1,128)}) custom-call(s32[1,1,8,16]{3,2,1,0:T(8,128)} %bitcast.17, s32[1,1,16]{2,1,0:T(1,128)} %counts.1, s32[1,1,1,8]{3,2,1,0:T(1,128)} %bitcast.19, s32[1,1,2,4]{3,2,1,0:T(2,128)} %bitcast.18, ...), custom_call_target="tpu_custom_call" | custom-call | tf_op jit(solution)/shard_map/gcn_layer/pallas_call | solution.py:353
  35.8 1.9 %copy.18 = bf16[2048,128]{1,0:T(8,128)(2,1)} copy(bf16[2048,128]{1,0:T(8,128)(2,1)} %bitcast.16) | data formatting | bytes 1048576
  37.7 1.9 %copy.19 = bf16[2048,128]{1,0:T(8,128)(2,1)} copy(bf16[2048,128]{1,0:T(8,128)(2,1)} %bitcast.15) | data formatting | bytes 1048576
  39.6 1.5 %copy.20 = f32[128,128]{1,0:T(8,128)} copy(f32[128,128]{1,0:T(8,128)} %get-tuple-element.18) | data formatting | bytes 131072
  41.0 1.2 %copy.21 = f32[128]{0:T(128)} copy(f32[128]{0:T(128)} %bitcast.21) | data formatting | bytes 1024
where the time goes:
time: 42.5 us; the launch traced here: 42.2 us
  Pallas kernels  35.2 us (83%)
  local copies, waits for them, and re-layouts  6.38 us (15%)
  between operations  0.64 us (2%)
    pallas_call x1, Pallas kernels, per_device(): pl.pallas_call(functools.partial(layer_kernel, (groups, members, rows, sl...  35.2 us
    unnamed x4, local copies, waits for them, and re-layouts  6.38 us

commit v1 on v0

--- a/solution.py
+++ b/solution.py
@@ -323,6 +323,15 @@
     bsum_ref[...] = result[0, share : share + 1]
 
 
+def push_kernel(out, grad, w_sum, b_sum, out_hbm, grad_hbm, w_hbm, b_hbm, sems):
+    pairs = ((out, out_hbm), (grad, grad_hbm), (w_sum, w_hbm), (b_sum, b_hbm))
+    copies = [pltpu.make_async_copy(a, b, sems.at[i]) for i, (a, b) in enumerate(pairs)]
+    for copy in copies:
+        copy.start()
+    for copy in copies:
+        copy.wait()
+
+
 def per_device(
     layer_input,
     history,
@@ -353,10 +362,10 @@
     out, grad, w_sum, b_sum = pl.pallas_call(
         functools.partial(layer_kernel, (groups, members, rows, slots, per_group, scale)),
         out_shape=(
-            jax.ShapeDtypeStruct(blocked, BF16),
-            jax.ShapeDtypeStruct(blocked, BF16),
-            jax.ShapeDtypeStruct((feats, feats), F32),
-            jax.ShapeDtypeStruct((1, feats), F32),
+            pltpu.VMEM(blocked, BF16),
+            pltpu.VMEM(blocked, BF16),
+            pltpu.VMEM((feats, feats), F32),
+            pltpu.VMEM((1, feats), F32),
         ),
         in_specs=[smem] * 4 + [hbm] * 4 + [vmem] * 2,
         out_specs=(vmem,) * 4,
@@ -392,20 +401,44 @@
             dma((groups,)),
         ],
         compiler_params=pltpu.CompilerParams(
-            collective_id=0, has_side_effects=True, vmem_limit_bytes=67043328
+            collective_id=0, has_side_effects=True, vmem_limit_bytes=50331648
         ),
         name="gcn_layer",
     )(
-        jnp.swapaxes(tile_source, 2, 3),
-        counts,
-        jnp.swapaxes(requests, 2, 3),
-        jnp.swapaxes(send_ids, 2, 3),
-        layer_input.reshape(blocked),
-        history.reshape(blocked),
-        adjacency.reshape(rows, slots, block, block),
-        cotangent.reshape(blocked),
-        weight,
-        layer_bias.reshape(1, feats),
+        *(
+            pltpu.with_memory_space_constraint(operand, pltpu.HBM)
+            for operand in (
+                jnp.swapaxes(tile_source, 2, 3),
+                counts,
+                jnp.swapaxes(requests, 2, 3),
+                jnp.swapaxes(send_ids, 2, 3),
+                layer_input.reshape(blocked),
+                history.reshape(blocked),
+                adjacency.reshape(rows, slots, block, block),
+                cotangent.reshape(blocked),
+                weight,
+                layer_bias.reshape(1, feats),
+            )
+        )
+    )
+    out, grad, w_sum, b_sum = pl.pallas_call(
+        push_kernel,
+        out_shape=(
+            jax.ShapeDtypeStruct(blocked, BF16),
+            jax.ShapeDtypeStruct(blocked, BF16),
+            jax.ShapeDtypeStruct((feats, feats), F32),
+            jax.ShapeDtypeStruct((1, feats), F32),
+        ),
+        in_specs=[vmem] * 4,
+        out_specs=(hbm,) * 4,
+        scratch_shapes=[dma((4,))],
+        compiler_params=pltpu.CompilerParams(vmem_limit_bytes=8388608),
+        name="push",
+    )(
+        *(
+            pltpu.with_memory_space_constraint(operand, pltpu.VMEM)
+            for operand in (out, grad, w_sum, b_sum)
+        )
     )
     return (
         out.reshape(-1, feats),

time: 42.5 us -> 36 us (0.85)
  local copies, waits for them, and re-layouts: 6.38 us -> 0 us
    unnamed x4 -> x0, local copies, waits for them, and re-layouts: 6.38 us -> none
    pallas_call x0 -> x1, Pallas kernels: none -> 1.01 us  [per_device(): pl.pallas_call(push_kernel, out_shape=(jax.ShapeDtypeStruct(blocked, BF16...]
    pallas_call x1, Pallas kernels: 35.2 us -> 34.2 us  [per_device(): pl.pallas_call(functools.partial(layer_kernel, (groups, members, rows, sl...]
where the time goes in v1:
time: 36 us; the launch traced here: 35.8 us
  Pallas kernels  35.2 us (98%)
  between operations  0.64 us (2%)
    pallas_call x1, Pallas kernels, per_device(): pl.pallas_call(functools.partial(layer_kernel, (groups, members, rows, sl...  34.2 us
    pallas_call x1, Pallas kernels, per_device(): pl.pallas_call(push_kernel, out_shape=(jax.ShapeDtypeStruct(blocked, BF16...  1.01 us

profile of v1, /device:TPU:0, one launch (start us, length us, event | category | flops | bytes accessed | tf_op | source)
XLA Modules:
  0.0 35.8 jit_solution(10588085412300963166)
XLA Ops:
  0.6 34.2 %gcn_layer.1 = (bf16[16,128,128]{2,1,0:T(8,128)(2,1)S(1)}, bf16[16,128,128]{2,1,0:T(8,128)(2,1)S(1)}, f32[128,128]{1,0:T(8,128)S(1)}, f32[1,128]{1,0:T(1,128)S(1)}) custom-call(s32[1,1,8,16]{3,2,1,0:T(8,128)} %bitcast.15, s32[1,1,16]{2,1,0:T(1,128)} %counts.1, s32[1,1,1,8]{3,2,1,0:T(1,128)} %bitcast.17, s32[1,1,2,4]{3,2,1,0:T(2,128)} %bitcast.16, ...), custom_call_target="tpu_custom_call" | custom-call | tf_op jit(solution)/shard_map/gcn_layer/pallas_call | solution.py:362
  34.8 1.0 %push.1 = (bf16[16,128,128]{2,1,0:T(8,128)(2,1)}, bf16[16,128,128]{2,1,0:T(8,128)(2,1)}, f32[128,128]{1,0:T(8,128)}, f32[1,128]{1,0:T(1,128)}) custom-call(bf16[16,128,128]{2,1,0:T(8,128)(2,1)S(1)} %get-tuple-element.12.out, bf16[16,128,128]{2,1,0:T(8,128)(2,1)S(1)} %get-tuple-element.13.grad, f32[128,128]{1,0:T(8,128)S(1)} %get-tuple-element.14.w_sum, ...), custom_call_target="tpu_custom_call" | custom-call | tf_op jit(solution)/shard_map/push/pallas_call | solution.py:424

commit v2 on v1

--- a/solution.py
+++ b/solution.py
@@ -13,8 +13,9 @@
 MESH = pl.DeviceIdType.MESH
 GELU_C = math.sqrt(2.0 / math.pi)
 GELU_A = 0.044715
-ROW_UNROLL = 4
-TILE_UNROLL = 4
+ROW_UNROLL = 8
+PAIR_UNROLL = 24
+CHUNK_ROWS = 2
 
 
 def dot(a, b, contract):
@@ -45,6 +46,8 @@
     inbox,
     served,
     outgoing,
+    agg,
+    grad_pre,
     grad_t,
     running,
     sort_vmem,
@@ -166,21 +169,34 @@
     across = jnp.broadcast_to(keys, (tiles, tiles))
     down = across.T
     place = lax.broadcasted_iota(jnp.int32, (tiles, tiles), 1)
+    across_to = across // tiles
+    down_to = down // tiles
 
     def count(where, axis):
         return jnp.sum(jnp.where(where, 1, 0), axis=axis, keepdims=True)
 
-    rank = count(across < down, 1)
-    first = count(across < (down // tiles) * tiles, 1)
-    placed = rank == place
-    below = count(down < place * tiles, 0)
-    upto = count(down < (place + 1) * tiles, 0)
-    sort_vmem[0:1, :] = jnp.sum(jnp.where(placed, down, 0), axis=0, keepdims=True)
-    sort_vmem[1:2, :] = jnp.where(upto > below, upto, 0)
-    sort_vmem[2:3, :] = count(placed & (rank > first), 0)
+    def pick(where, value):
+        return jnp.sum(jnp.where(where, value, 0), axis=0, keepdims=True)
+
+    within_across = count(down < across, 0) - count(down < across_to * tiles, 0)
+    within = count(across < down, 1) - count(across < down_to * tiles, 1)
+    leads = within_across % 2 == 0
+    pair = count(leads & (across_to < down_to), 1) + within // 2
+    here = (pair == place) & (down_to < rows)
+    lead = within % 2 == 0
+    upto = count(lead & (down_to <= place), 0)
+    mine = count(down_to == place, 0)
+    tile = down % tiles
+    sort_vmem[0:1, :] = pick(here & lead, tile // slots + 1)
+    sort_vmem[1:2, :] = pick(here & lead, tile)
+    sort_vmem[2:3, :] = pick(here & (within % 2 == 1), tile // slots + 1)
+    sort_vmem[3:4, :] = pick(here & (within % 2 == 1), tile)
+    sort_vmem[4:5, :] = pick(here & lead & (within > 0), 1)
+    sort_vmem[5:6, :] = jnp.where(mine > 0, upto, 0)
     sort_copy = pltpu.make_async_copy(sort_vmem, sort_smem, local_sem.at[4])
     sort_copy.start()
     running[0] = jnp.zeros((feats, block), F32)
+    grad_t[0] = jnp.zeros((feats, block), BF16)
 
     x_copy.wait()
     adj_copy.wait()
@@ -193,42 +209,43 @@
         peer = mem_peer(step)
         fetch_copy(peer, peer).wait_recv()
 
-    def forward(r, live):
+    def gather_row(r):
+        live = counts[0, 0, r]
         sources = []
         for k in range(slots):
             at = jnp.where(k < live, tile_source[0, 0, k, r], zero_block)
             sources.append(table[at])
         wide = jnp.concatenate([adj[r, k] for k in range(slots)], axis=1)
         tall = jnp.concatenate(sources, axis=0)
-        agg = dot(wide, tall, ((1,), (0,))).astype(BF16)
-        pre = dot(agg, weight[...], ((1,), (0,))) + bias[...]
+        agg[r] = dot(wide, tall, ((1,), (0,))).astype(BF16)
+
+    def gather_rows(i, carry):
+        for u in range(ROW_UNROLL):
+            gather_row(i * ROW_UNROLL + u)
+        return carry
+
+    lax.fori_loop(0, rows // ROW_UNROLL, gather_rows, jnp.int32(0))
+
+    nodes = CHUNK_ROWS * block
+
+    def activate(r):
+        rows_here = agg[pl.ds(r, CHUNK_ROWS)].reshape(nodes, feats)
+        pre = dot(rows_here, weight[...], ((1,), (0,))) + bias[...]
         square = pre * pre
         t = jnp.tanh(GELU_C * (pre + GELU_A * (square * pre)))
         half = 0.5 * (1.0 + t)
-        out_ref[r] = (pre * half).astype(BF16)
+        out_ref[pl.ds(r, CHUNK_ROWS)] = (pre * half).astype(BF16).reshape(CHUNK_ROWS, block, feats)
         slope = half + (0.5 * pre) * (1.0 - t * t) * (GELU_C * (1.0 + (3.0 * GELU_A) * square))
-        grad_pre = (cot[r].astype(F32) * slope).astype(BF16)
-        grad_t[r] = dot(weight[...], grad_pre, ((1,), (1,))).astype(BF16)
-        return (
-            dot(agg, grad_pre, ((0,), (0,))),
-            jnp.sum(grad_pre.astype(F32), axis=0, keepdims=True),
-        )
-
-    def forward_rows(i, carry):
-        w_sum, b_sum = carry
-        for u in range(ROW_UNROLL):
-            r = i * ROW_UNROLL + u
-            w_part, b_part = forward(r, counts[0, 0, r])
-            w_sum = w_sum + w_part
-            b_sum = b_sum + b_part
-        return w_sum, b_sum
-
-    w_sum, b_sum = lax.fori_loop(
-        0,
-        rows // ROW_UNROLL,
-        forward_rows,
-        (jnp.zeros((feats, feats), F32), jnp.zeros((1, feats), F32)),
-    )
+        cots = cot[pl.ds(r, CHUNK_ROWS)].reshape(nodes, feats).astype(F32)
+        grads = (cots * slope).astype(BF16)
+        grad_pre[pl.ds(r, CHUNK_ROWS)] = grads.reshape(CHUNK_ROWS, block, feats)
+        return jnp.sum(grads.astype(F32), axis=0, keepdims=True)
+
+    b_sum = jnp.zeros((1, feats), F32)
+    for i in range(rows // CHUNK_ROWS):
+        b_sum = b_sum + activate(i * CHUNK_ROWS)
+    whole = (rows * block, feats)
+    w_sum = dot(agg[...].reshape(whole), grad_pre[...].reshape(whole), ((0,), (0,)))
 
     share = feats // groups
     for g in range(groups):
@@ -269,17 +286,28 @@
         a_copy(g_me, grp_peer(step)).start()
     scattered[g_me] = parts[g_me]
 
-    def backward_tiles(i, carry):
-        for u in range(TILE_UNROLL):
-            p = i * TILE_UNROLL + u
-            key = sort_smem[0, p]
-            j = key % tiles
-            term = dot(grad_t[j // slots], adj[j // slots, j % slots], ((1,), (0,)))
-            running[p + 1] = term + jnp.where(sort_smem[2, p] > 0, running[p], 0.0)
-        return carry
-
-    trips = tiles // TILE_UNROLL
-    carry = lax.fori_loop(0, trips // 2, backward_tiles, jnp.int32(0))
+    for i in range(rows // CHUNK_ROWS):
+        grads = grad_pre[pl.ds(i * CHUNK_ROWS, CHUNK_ROWS)].reshape(nodes, feats)
+        flipped = dot(weight[...], grads, ((1,), (1,))).astype(BF16)
+        for u in range(CHUNK_ROWS):
+            grad_t[i * CHUNK_ROWS + u + 1] = flipped[:, u * block : (u + 1) * block]
+
+    def backward_pairs(i, total):
+        for u in range(PAIR_UNROLL):
+            p = i * PAIR_UNROLL + u
+            first = sort_smem[1, p]
+            second = sort_smem[3, p]
+            wide = jnp.concatenate([grad_t[sort_smem[0, p]], grad_t[sort_smem[2, p]]], axis=1)
+            tall = jnp.concatenate(
+                [adj[first // slots, first % slots], adj[second // slots, second % slots]], axis=0
+            )
+            term = dot(wide, tall, ((1,), (0,)))
+            total = term + jnp.where(sort_smem[4, p] > 0, total, 0.0)
+            running[p + 1] = total
+        return total
+
+    trips = (tiles + rows) // 2 // PAIR_UNROLL
+    lax.fori_loop(0, trips, backward_pairs, jnp.zeros((feats, block), F32))
 
     for step in range(1, groups):
         peer = grp_peer(step)
@@ -291,9 +319,8 @@
     for step in range(1, members):
         b_copy(m_me, mem_peer(step)).start()
 
-    carry = lax.fori_loop(trips // 2, trips, backward_tiles, carry)
     for c in range(rows):
-        grad_ref[c] = running[sort_smem[1, c]].T.astype(BF16)
+        grad_ref[c] = running[sort_smem[5, c]].T.astype(BF16)
 
     for step in range(1, members):
         peer = mem_peer(step)
@@ -351,6 +378,7 @@
     per_group = send_ids.shape[3]
     assert requests.shape[3] == 1
     tiles = rows * slots
+    assert rows % ROW_UNROLL == 0 and (tiles + rows) % (2 * PAIR_UNROLL) == 0
     scale = (layer_input.shape[0] * groups * members) ** (-0.5)
     share = feats // groups + 8
     sources = rows + members + groups * per_group + 1
@@ -378,8 +406,10 @@
             pltpu.VMEM((members, 8, 128), jnp.int32),
             pltpu.VMEM((members, block, feats), BF16),
             pltpu.VMEM((groups, per_group, block, feats), BF16),
-            pltpu.VMEM((rows, feats, block), BF16),
-            pltpu.VMEM((tiles + 1, feats, block), F32),
+            pltpu.VMEM(blocked, BF16),
+            pltpu.VMEM(blocked, BF16),
+            pltpu.VMEM((rows + 1, feats, block), BF16),
+            pltpu.VMEM(((tiles + rows) // 2 + 1, feats, block), F32),
             pltpu.VMEM((8, tiles), jnp.int32),
             pltpu.SMEM((8, tiles), jnp.int32),
             pltpu.VMEM((groups, share, feats), F32),

time: 36 us -> 31.9 us (0.89)
  Pallas kernels: 35.2 us -> 31.1 us
    pallas_call x1, Pallas kernels: 34.2 us -> 30.1 us  [per_device(): pl.pallas_call(functools.partial(layer_kernel, (groups, members, rows, sl...]
where the time goes in v2:
time: 31.9 us; the launch traced here: 31.7 us
  Pallas kernels  31.1 us (97%)
  between operations  0.64 us (2%)
    pallas_call x1, Pallas kernels, per_device(): pl.pallas_call(functools.partial(layer_kernel, (groups, members, rows, sl...  30.1 us
    pallas_call x1, Pallas kernels, per_device(): pl.pallas_call(push_kernel, out_shape=(jax.ShapeDtypeStruct(blocked, BF16...  1.01 us

profile of v2, /device:TPU:0, one launch (start us, length us, event | category | flops | bytes accessed | tf_op | source)
XLA Modules:
  0.0 31.7 jit_solution(402686332888309187)
XLA Ops:
  0.6 30.1 %gcn_layer.1 = (bf16[16,128,128]{2,1,0:T(8,128)(2,1)S(1)}, bf16[16,128,128]{2,1,0:T(8,128)(2,1)S(1)}, f32[128,128]{1,0:T(8,128)S(1)}, f32[1,128]{1,0:T(1,128)S(1)}) custom-call(s32[1,1,8,16]{3,2,1,0:T(8,128)} %bitcast.15, s32[1,1,16]{2,1,0:T(1,128)} %counts.1, s32[1,1,1,8]{3,2,1,0:T(1,128)} %bitcast.17, s32[1,1,2,4]{3,2,1,0:T(2,128)} %bitcast.16, ...), custom_call_target="tpu_custom_call" | custom-call | tf_op jit(solution)/shard_map/gcn_layer/pallas_call | solution.py:390
  30.7 1.0 %push.1 = (bf16[16,128,128]{2,1,0:T(8,128)(2,1)}, bf16[16,128,128]{2,1,0:T(8,128)(2,1)}, f32[128,128]{1,0:T(8,128)}, f32[1,128]{1,0:T(1,128)}) custom-call(bf16[16,128,128]{2,1,0:T(8,128)(2,1)S(1)} %get-tuple-element.12.out, bf16[16,128,128]{2,1,0:T(8,128)(2,1)S(1)} %get-tuple-element.13.grad, f32[128,128]{1,0:T(8,128)S(1)} %get-tuple-element.14.w_sum, ...), custom_call_target="tpu_custom_call" | custom-call | tf_op jit(solution)/shard_map/push/pallas_call | solution.py:454

commit v3 on v2

--- a/solution.py
+++ b/solution.py
@@ -13,7 +13,6 @@
 MESH = pl.DeviceIdType.MESH
 GELU_C = math.sqrt(2.0 / math.pi)
 GELU_A = 0.044715
-ROW_UNROLL = 8
 PAIR_UNROLL = 24
 CHUNK_ROWS = 2
 
@@ -46,7 +45,6 @@
     inbox,
     served,
     outgoing,
-    agg,
     grad_pre,
     grad_t,
     running,
@@ -54,7 +52,6 @@
     sort_smem,
     parts,
     scattered,
-    gathered,
     result,
     local_sem,
     req_send,
@@ -67,11 +64,11 @@
     a_recv,
     b_send,
     b_recv,
-    c_send,
-    c_recv,
 ):
-    groups, members, rows, slots, per_group, scale = dims
+    groups, members, rows, slots, per_group, scale, first_owner, span = dims
     tiles = rows * slots
+    owners = groups * span
+    share = weight.shape[0] // owners
     g_me = lax.axis_index("grp")
     m_me = lax.axis_index("mem")
     block = hist.shape[1]
@@ -81,6 +78,14 @@
 
     def mem_peer(step):
         return lax.rem(m_me + step, members)
+
+    low = jnp.minimum(m_me, members - 1 - m_me)
+    parity = 1 - 2 * lax.rem(m_me, 2)
+    inward = jnp.where(2 * m_me < members - 1, 1, -1)
+
+    def near_peer(step):
+        both_sides = (step + 1) // 2 * (1 if step % 2 else -1)
+        return m_me + jnp.where(step <= 2 * low, parity * both_sides, inward * (step - low))
 
     def grp_peer(step):
         return lax.rem(g_me + step, groups)
@@ -102,10 +107,6 @@
     for m in range(members):
         outbox[m] = jnp.full(outbox.shape[1:], requests[0, 0, 0, m], jnp.int32)
     table[zero_block] = jnp.zeros((block, feats), BF16)
-    hist_copy.wait()
-    for g in range(groups):
-        for b in range(per_group):
-            outgoing[g, b] = hist[send_ids[0, 0, b, g]]
     pl.semaphore_wait(barrier, members + groups - 2)
 
     def req_copy(slot_there, peer):
@@ -139,7 +140,11 @@
         )
 
     for step in range(1, members):
-        req_copy(m_me, mem_peer(step)).start()
+        req_copy(m_me, near_peer(members - step)).start()
+    hist_copy.wait()
+    for g in range(groups):
+        for b in range(per_group):
+            outgoing[g, b] = hist[send_ids[0, 0, b, g]]
     for step in range(1, groups):
         border_copy(g_me, grp_peer(step)).start()
 
@@ -148,7 +153,7 @@
         table[border_at + g_me * per_group + b] = hist[send_ids[0, 0, b, g_me]]
 
     for step in range(1, members):
-        peer = mem_peer(step)
+        peer = near_peer(step)
         req_copy(peer, peer).wait_recv()
         wanted = inbox[peer][0, 0]
         served[peer] = hist[wanted]
@@ -217,20 +222,12 @@
             sources.append(table[at])
         wide = jnp.concatenate([adj[r, k] for k in range(slots)], axis=1)
         tall = jnp.concatenate(sources, axis=0)
-        agg[r] = dot(wide, tall, ((1,), (0,))).astype(BF16)
-
-    def gather_rows(i, carry):
-        for u in range(ROW_UNROLL):
-            gather_row(i * ROW_UNROLL + u)
-        return carry
-
-    lax.fori_loop(0, rows // ROW_UNROLL, gather_rows, jnp.int32(0))
+        return dot(wide, tall, ((1,), (0,))).astype(BF16)
 
     nodes = CHUNK_ROWS * block
 
-    def activate(r):
-        rows_here = agg[pl.ds(r, CHUNK_ROWS)].reshape(nodes, feats)
-        pre = dot(rows_here, weight[...], ((1,), (0,))) + bias[...]
+    def activate(r, agg):
+        pre = dot(agg, weight[...], ((1,), (0,))) + bias[...]
         square = pre * pre
         t = jnp.tanh(GELU_C * (pre + GELU_A * (square * pre)))
         half = 0.5 * (1.0 + t)
@@ -239,52 +236,58 @@
         cots = cot[pl.ds(r, CHUNK_ROWS)].reshape(nodes, feats).astype(F32)
         grads = (cots * slope).astype(BF16)
         grad_pre[pl.ds(r, CHUNK_ROWS)] = grads.reshape(CHUNK_ROWS, block, feats)
-        return jnp.sum(grads.astype(F32), axis=0, keepdims=True)
-
+        w_part = dot(agg, grads, ((0,), (0,)))
+        return w_part, jnp.sum(grads.astype(F32), axis=0, keepdims=True)
+
+    def gather_chunk(i):
+        return jnp.concatenate([gather_row(i * CHUNK_ROWS + u) for u in range(CHUNK_ROWS)], axis=0)
+
+    w_sum = jnp.zeros((feats, feats), F32)
     b_sum = jnp.zeros((1, feats), F32)
-    for i in range(rows // CHUNK_ROWS):
-        b_sum = b_sum + activate(i * CHUNK_ROWS)
-    whole = (rows * block, feats)
-    w_sum = dot(agg[...].reshape(whole), grad_pre[...].reshape(whole), ((0,), (0,)))
-
-    share = feats // groups
-    for g in range(groups):
-        parts[g, 0:share] = w_sum[g * share : (g + 1) * share]
-        parts[g, share : share + 8] = jnp.broadcast_to(b_sum, (8, feats))
-
-    def a_copy(slot_there, peer):
+    chunks = rows // CHUNK_ROWS
+    held = gather_chunk(0)
+    for i in range(chunks):
+        following = gather_chunk(i + 1) if i + 1 < chunks else None
+        w_part, b_part = activate(i * CHUNK_ROWS, held)
+        w_sum = w_sum + w_part
+        b_sum = b_sum + b_part
+        held = following
+
+    send_rows = pl.ds(0, share + 1)
+    for o in range(owners):
+        parts[o, 0:share] = w_sum[o * share : (o + 1) * share]
+        parts[o, share : share + 1] = b_sum
+    me = g_me * members + m_me
+    devices = groups * members
+    owning = (m_me >= first_owner) & (m_me < first_owner + span)
+    own = g_me * span + jnp.clip(m_me - first_owner, 0, span - 1)
+
+    def a_copy(owner, sender):
         return pltpu.make_async_remote_copy(
-            src_ref=parts.at[peer],
-            dst_ref=scattered.at[slot_there],
-            send_sem=a_send.at[peer],
-            recv_sem=a_recv.at[slot_there],
-            device_id={"grp": peer},
+            src_ref=parts.at[owner, send_rows],
+            dst_ref=scattered.at[sender, send_rows],
+            send_sem=a_send.at[owner],
+            recv_sem=a_recv.at[sender],
+            device_id={"grp": owner // span, "mem": first_owner + lax.rem(owner, span)},
             device_id_type=MESH,
         )
 
-    def b_copy(slot_there, peer):
+    def b_copy(owner, device):
         return pltpu.make_async_remote_copy(
-            src_ref=gathered.at[m_me],
-            dst_ref=gathered.at[slot_there],
-            send_sem=b_send.at[peer],
-            recv_sem=b_recv.at[slot_there],
-            device_id={"mem": peer},
+            src_ref=result.at[owner, send_rows],
+            dst_ref=result.at[owner, send_rows],
+            send_sem=b_send.at[device],
+            recv_sem=b_recv.at[owner],
+            device_id={"grp": device // members, "mem": lax.rem(device, members)},
             device_id_type=MESH,
         )
 
-    def c_copy(slot_there, peer):
-        return pltpu.make_async_remote_copy(
-            src_ref=result.at[g_me],
-            dst_ref=result.at[slot_there],
-            send_sem=c_send.at[peer],
-            recv_sem=c_recv.at[slot_there],
-            device_id={"grp": peer},
-            device_id_type=MESH,
-        )
-
-    for step in range(1, groups):
-        a_copy(g_me, grp_peer(step)).start()
-    scattered[g_me] = parts[g_me]
+    for step in range(1, owners):
+        a_copy(lax.rem(own + step, owners), me).start()
+
+    @pl.when(jnp.logical_not(owning))
+    def _():
+        a_copy(own, me).start()
 
     for i in range(rows // CHUNK_ROWS):
         grads = grad_pre[pl.ds(i * CHUNK_ROWS, CHUNK_ROWS)].reshape(nodes, feats)
@@ -309,45 +312,46 @@
     trips = (tiles + rows) // 2 // PAIR_UNROLL
     lax.fori_loop(0, trips, backward_pairs, jnp.zeros((feats, block), F32))
 
-    for step in range(1, groups):
-        peer = grp_peer(step)
-        a_copy(peer, peer).wait_recv()
-    chunk = scattered[0]
-    for g in range(1, groups):
-        chunk = chunk + scattered[g]
-    gathered[m_me] = chunk
-    for step in range(1, members):
-        b_copy(m_me, mem_peer(step)).start()
-
     for c in range(rows):
         grad_ref[c] = running[sort_smem[5, c]].T.astype(BF16)
 
-    for step in range(1, members):
-        peer = mem_peer(step)
-        b_copy(peer, peer).wait_recv()
-    chunk = gathered[0]
-    for m in range(1, members):
-        chunk = chunk + gathered[m]
-    result[g_me] = chunk * scale
-    for step in range(1, groups):
-        c_copy(g_me, grp_peer(step)).start()
+    @pl.when(owning)
+    def _():
+        scattered[me] = parts[own]
+        for step in range(1, devices):
+            a_copy(own, lax.rem(me + step, devices)).wait_recv()
+        chunk = scattered[0]
+        for d in range(1, devices):
+            chunk = chunk + scattered[d]
+        result[own] = chunk * scale
+        for step in range(1, devices):
+            b_copy(own, lax.rem(me + step, devices)).start()
 
     for step in range(1, members):
         peer = mem_peer(step)
         req_copy(m_me, peer).wait_send()
         fetch_copy(m_me, peer).wait_send()
-        b_copy(m_me, peer).wait_send()
     for step in range(1, groups):
-        peer = grp_peer(step)
-        border_copy(g_me, peer).wait_send()
-        a_copy(g_me, peer).wait_send()
-        c_copy(g_me, peer).wait_send()
-    for step in range(1, groups):
-        peer = grp_peer(step)
-        c_copy(peer, peer).wait_recv()
-    for g in range(groups):
-        wsum_ref[g * share : (g + 1) * share] = result[g, 0:share]
+        border_copy(g_me, grp_peer(step)).wait_send()
+    for step in range(1, owners):
+        a_copy(lax.rem(own + step, owners), me).wait_send()
+
+    @pl.when(jnp.logical_not(owning))
+    def _():
+        a_copy(own, me).wait_send()
+        b_copy(own, me).wait_recv()
+
+    for step in range(1, owners):
+        b_copy(lax.rem(own + step, owners), me).wait_recv()
+
+    for o in range(owners):
+        wsum_ref[o * share : (o + 1) * share] = result[o, 0:share]
     bsum_ref[...] = result[0, share : share + 1]
+
+    @pl.when(owning)
+    def _():
+        for step in range(1, devices):
+            b_copy(own, lax.rem(me + step, devices)).wait_send()
 
 
 def push_kernel(out, grad, w_sum, b_sum, out_hbm, grad_hbm, w_hbm, b_hbm, sems):
@@ -378,9 +382,12 @@
     per_group = send_ids.shape[3]
     assert requests.shape[3] == 1
     tiles = rows * slots
-    assert rows % ROW_UNROLL == 0 and (tiles + rows) % (2 * PAIR_UNROLL) == 0
+    assert rows % CHUNK_ROWS == 0 and (tiles + rows) % (2 * PAIR_UNROLL) == 0
     scale = (layer_input.shape[0] * groups * members) ** (-0.5)
-    share = feats // groups + 8
+    span = next(n for n in range(max(members // 2, 1), 0, -1) if feats % (groups * n) == 0)
+    first_owner = (members - span) // 2
+    owners = groups * span
+    padded = (feats // owners) // 8 * 8 + 8
     sources = rows + members + groups * per_group + 1
     blocked = (rows, block, feats)
     dma = pltpu.SemaphoreType.DMA
@@ -388,7 +395,7 @@
     vmem = pl.BlockSpec(memory_space=pltpu.VMEM)
     hbm = pl.BlockSpec(memory_space=pltpu.HBM)
     out, grad, w_sum, b_sum = pl.pallas_call(
-        functools.partial(layer_kernel, (groups, members, rows, slots, per_group, scale)),
+        functools.partial(layer_kernel, (groups, members, rows, slots, per_group, scale, first_owner, span)),
         out_shape=(
             pltpu.VMEM(blocked, BF16),
             pltpu.VMEM(blocked, BF16),
@@ -402,20 +409,18 @@
             pltpu.VMEM(blocked, BF16),
             pltpu.VMEM((rows, slots, block, block), BF16),
             pltpu.VMEM(blocked, BF16),
-            pltpu.VMEM((members, 8, 128), jnp.int32),
-            pltpu.VMEM((members, 8, 128), jnp.int32),
+            pltpu.VMEM((members, 1, 128), jnp.int32),
+            pltpu.VMEM((members, 1, 128), jnp.int32),
             pltpu.VMEM((members, block, feats), BF16),
             pltpu.VMEM((groups, per_group, block, feats), BF16),
-            pltpu.VMEM(blocked, BF16),
             pltpu.VMEM(blocked, BF16),
             pltpu.VMEM((rows + 1, feats, block), BF16),
             pltpu.VMEM(((tiles + rows) // 2 + 1, feats, block), F32),
             pltpu.VMEM((8, tiles), jnp.int32),
             pltpu.SMEM((8, tiles), jnp.int32),
-            pltpu.VMEM((groups, share, feats), F32),
-            pltpu.VMEM((groups, share, feats), F32),
-            pltpu.VMEM((members, share, feats), F32),
-            pltpu.VMEM((groups, share, feats), F32),
+            pltpu.VMEM((owners, padded, feats), F32),
+            pltpu.VMEM((groups * members, padded, feats), F32),
+            pltpu.VMEM((owners, padded, feats), F32),
             dma((5,)),
             dma((members,)),
             dma((members,)),
@@ -423,12 +428,10 @@
             dma((members,)),
             dma((groups,)),
             dma((groups,)),
-            dma((groups,)),
-            dma((groups,)),
-            dma((members,)),
-            dma((members,)),
-            dma((groups,)),
-            dma((groups,)),
+            dma((owners,)),
+            dma((groups * members,)),
+            dma((groups * members,)),
+            dma((owners,)),
         ],
         compiler_params=pltpu.CompilerParams(
             collective_id=0, has_side_effects=True, vmem_limit_bytes=50331648

time: 31.9 us -> 31 us (0.972)
  Pallas kernels: 31.1 us -> 30.2 us
    pallas_call x1, Pallas kernels: 30.1 us -> 29.2 us  [per_device(): pl.pallas_call(functools.partial(layer_kernel, (groups, members, rows, sl...]
where the time goes in v3:
time: 31 us; the launch traced here: 30.9 us
  Pallas kernels  30.2 us (97%)
  between operations  0.64 us (2%)
    pallas_call x1, Pallas kernels, per_device(): pl.pallas_call(functools.partial(layer_kernel, (groups, members, rows, sl...  29.2 us
    pallas_call x1, Pallas kernels, per_device(): pl.pallas_call(push_kernel, out_shape=(jax.ShapeDtypeStruct(blocked, BF16...  1.01 us

profile of v3, /device:TPU:0, one launch (start us, length us, event | category | flops | bytes accessed | tf_op | source)
XLA Modules:
  0.0 30.9 jit_solution(12564622315233654075)
XLA Ops:
  0.6 29.2 %gcn_layer.1 = (bf16[16,128,128]{2,1,0:T(8,128)(2,1)S(1)}, bf16[16,128,128]{2,1,0:T(8,128)(2,1)S(1)}, f32[128,128]{1,0:T(8,128)S(1)}, f32[1,128]{1,0:T(1,128)S(1)}) custom-call(s32[1,1,8,16]{3,2,1,0:T(8,128)} %bitcast.15, s32[1,1,16]{2,1,0:T(1,128)} %counts.1, s32[1,1,1,8]{3,2,1,0:T(1,128)} %bitcast.17, s32[1,1,2,4]{3,2,1,0:T(2,128)} %bitcast.16, ...), custom_call_target="tpu_custom_call" | custom-call | tf_op jit(solution)/shard_map/gcn_layer/pallas_call | solution.py:397
  29.8 1.0 %push.1 = (bf16[16,128,128]{2,1,0:T(8,128)(2,1)}, bf16[16,128,128]{2,1,0:T(8,128)(2,1)}, f32[128,128]{1,0:T(8,128)}, f32[1,128]{1,0:T(1,128)}) custom-call(bf16[16,128,128]{2,1,0:T(8,128)(2,1)S(1)} %get-tuple-element.12.out, bf16[16,128,128]{2,1,0:T(8,128)(2,1)S(1)} %get-tuple-element.13.grad, f32[128,128]{1,0:T(8,128)S(1)} %get-tuple-element.14.w_sum, ...), custom_call_target="tpu_custom_call" | custom-call | tf_op jit(solution)/shard_map/push/pallas_call | solution.py:457

commit v4 on v3

--- a/solution.py
+++ b/solution.py
@@ -14,7 +14,7 @@
 GELU_C = math.sqrt(2.0 / math.pi)
 GELU_A = 0.044715
 PAIR_UNROLL = 24
-CHUNK_ROWS = 2
+CHUNK_ROWS = 4
 
 
 def dot(a, b, contract):
@@ -53,6 +53,8 @@
     parts,
     scattered,
     result,
+    bias_mine,
+    bias_parts,
     local_sem,
     req_send,
     req_recv,
@@ -64,10 +66,12 @@
     a_recv,
     b_send,
     b_recv,
+    bias_send,
+    bias_recv,
 ):
-    groups, members, rows, slots, per_group, scale, first_owner, span = dims
+    groups, members, rows, slots, per_group, scale, first_owner, span, stride = dims
     tiles = rows * slots
-    owners = groups * span
+    owners = groups // stride * span
     share = weight.shape[0] // owners
     g_me = lax.axis_index("grp")
     m_me = lax.axis_index("mem")
@@ -229,10 +233,11 @@
     def activate(r, agg):
         pre = dot(agg, weight[...], ((1,), (0,))) + bias[...]
         square = pre * pre
-        t = jnp.tanh(GELU_C * (pre + GELU_A * (square * pre)))
-        half = 0.5 * (1.0 + t)
+        t = jnp.tanh(pre * (GELU_C + (GELU_C * GELU_A) * square))
+        half = 0.5 + 0.5 * t
         out_ref[pl.ds(r, CHUNK_ROWS)] = (pre * half).astype(BF16).reshape(CHUNK_ROWS, block, feats)
-        slope = half + (0.5 * pre) * (1.0 - t * t) * (GELU_C * (1.0 + (3.0 * GELU_A) * square))
+        rise = 2.0 * GELU_C + (6.0 * GELU_C * GELU_A) * square
+        slope = half + half * (((1.0 - half) * pre) * rise)
         cots = cot[pl.ds(r, CHUNK_ROWS)].reshape(nodes, feats).astype(F32)
         grads = (cots * slope).astype(BF16)
         grad_pre[pl.ds(r, CHUNK_ROWS)] = grads.reshape(CHUNK_ROWS, block, feats)
@@ -253,41 +258,60 @@
         b_sum = b_sum + b_part
         held = following
 
-    send_rows = pl.ds(0, share + 1)
+    padding = jnp.zeros((parts.shape[1] - share, feats), F32)
     for o in range(owners):
-        parts[o, 0:share] = w_sum[o * share : (o + 1) * share]
-        parts[o, share : share + 1] = b_sum
+        part = w_sum[o * share : (o + 1) * share]
+        if parts.shape[1] > share:
+            part = jnp.concatenate([part, padding], axis=0)
+        parts[o] = part.astype(BF16)
     me = g_me * members + m_me
     devices = groups * members
-    owning = (m_me >= first_owner) & (m_me < first_owner + span)
-    own = g_me * span + jnp.clip(m_me - first_owner, 0, span - 1)
+    owning = (lax.rem(g_me, stride) == stride - 1) & (m_me >= first_owner) & (m_me < first_owner + span)
+    own = g_me // stride * span + jnp.clip(m_me - first_owner, 0, span - 1)
 
     def a_copy(owner, sender):
         return pltpu.make_async_remote_copy(
-            src_ref=parts.at[owner, send_rows],
-            dst_ref=scattered.at[sender, send_rows],
+            src_ref=parts.at[owner],
+            dst_ref=scattered.at[sender],
             send_sem=a_send.at[owner],
             recv_sem=a_recv.at[sender],
-            device_id={"grp": owner // span, "mem": first_owner + lax.rem(owner, span)},
+            device_id={
+                "grp": owner // span * stride + stride - 1,
+                "mem": first_owner + lax.rem(owner, span),
+            },
             device_id_type=MESH,
         )
 
     def b_copy(owner, device):
         return pltpu.make_async_remote_copy(
-            src_ref=result.at[owner, send_rows],
-            dst_ref=result.at[owner, send_rows],
+            src_ref=result.at[owner],
+            dst_ref=result.at[owner],
             send_sem=b_send.at[device],
             recv_sem=b_recv.at[owner],
             device_id={"grp": device // members, "mem": lax.rem(device, members)},
             device_id_type=MESH,
         )
 
+    def bias_copy(slot_there, device):
+        return pltpu.make_async_remote_copy(
+            src_ref=bias_mine,
+            dst_ref=bias_parts.at[slot_there],
+            send_sem=bias_send.at[device],
+            recv_sem=bias_recv.at[slot_there],
+            device_id={"grp": device // members, "mem": lax.rem(device, members)},
+            device_id_type=MESH,
+        )
+
     for step in range(1, owners):
         a_copy(lax.rem(own + step, owners), me).start()
 
     @pl.when(jnp.logical_not(owning))
     def _():
         a_copy(own, me).start()
+
+    bias_mine[...] = b_sum
+    for step in range(1, devices):
+        bias_copy(me, lax.rem(me + step, devices)).start()
 
     for i in range(rows // CHUNK_ROWS):
         grads = grad_pre[pl.ds(i * CHUNK_ROWS, CHUNK_ROWS)].reshape(nodes, feats)
@@ -320,10 +344,10 @@
         scattered[me] = parts[own]
         for step in range(1, devices):
             a_copy(own, lax.rem(me + step, devices)).wait_recv()
-        chunk = scattered[0]
+        chunk = scattered[0].astype(F32)
         for d in range(1, devices):
-            chunk = chunk + scattered[d]
-        result[own] = chunk * scale
+            chunk = chunk + scattered[d].astype(F32)
+        result[own] = (chunk * scale).astype(BF16)
         for step in range(1, devices):
             b_copy(own, lax.rem(me + step, devices)).start()
 
@@ -341,12 +365,20 @@
         a_copy(own, me).wait_send()
         b_copy(own, me).wait_recv()
 
+    bias_parts[me] = bias_mine[...]
+    for step in range(1, devices):
+        bias_copy(lax.rem(me + step, devices), me).wait_recv()
+        bias_copy(me, lax.rem(me + step, devices)).wait_send()
+    b_total = bias_parts[0]
+    for d in range(1, devices):
+        b_total = b_total + bias_parts[d]
+    bsum_ref[...] = b_total * scale
+
     for step in range(1, owners):
         b_copy(lax.rem(own + step, owners), me).wait_recv()
 
     for o in range(owners):
-        wsum_ref[o * share : (o + 1) * share] = result[o, 0:share]
-    bsum_ref[...] = result[0, share : share + 1]
+        wsum_ref[o * share : (o + 1) * share] = result[o].astype(F32)[0:share]
 
     @pl.when(owning)
     def _():
@@ -384,10 +416,13 @@
     tiles = rows * slots
     assert rows % CHUNK_ROWS == 0 and (tiles + rows) % (2 * PAIR_UNROLL) == 0
     scale = (layer_input.shape[0] * groups * members) ** (-0.5)
-    span = next(n for n in range(max(members // 2, 1), 0, -1) if feats % (groups * n) == 0)
+    stride = 2 if groups % 2 == 0 else 1
+    columns = groups // stride
+    span = next(n for n in range(max(members // 2, 1), 0, -1) if feats % (columns * n) == 0)
     first_owner = (members - span) // 2
-    owners = groups * span
-    padded = (feats // owners) // 8 * 8 + 8
+    owners = columns * span
+    devices = groups * members
+    padded = (feats // owners + 7) // 8 * 8
     sources = rows + members + groups * per_group + 1
     blocked = (rows, block, feats)
     dma = pltpu.SemaphoreType.DMA
@@ -395,7 +430,7 @@
     vmem = pl.BlockSpec(memory_space=pltpu.VMEM)
     hbm = pl.BlockSpec(memory_space=pltpu.HBM)
     out, grad, w_sum, b_sum = pl.pallas_call(
-        functools.partial(layer_kernel, (groups, members, rows, slots, per_group, scale, first_owner, span)),
+        functools.partial(layer_kernel, (groups, members, rows, slots, per_group, scale, first_owner, span, stride)),
         out_shape=(
             pltpu.VMEM(blocked, BF16),
             pltpu.VMEM(blocked, BF16),
@@ -418,9 +453,11 @@
             pltpu.VMEM(((tiles + rows) // 2 + 1, feats, block), F32),
             pltpu.VMEM((8, tiles), jnp.int32),
             pltpu.SMEM((8, tiles), jnp.int32),
-            pltpu.VMEM((owners, padded, feats), F32),
-            pltpu.VMEM((groups * members, padded, feats), F32),
-            pltpu.VMEM((owners, padded, feats), F32),
+            pltpu.VMEM((owners, padded, feats), BF16),
+            pltpu.VMEM((devices, padded, feats), BF16),
+            pltpu.VMEM((owners, padded, feats), BF16),
+            pltpu.VMEM((1, feats), F32),
+            pltpu.VMEM((devices, 1, feats), F32),
             dma((5,)),
             dma((members,)),
             dma((members,)),
@@ -429,9 +466,11 @@
             dma((groups,)),
             dma((groups,)),
             dma((owners,)),
-            dma((groups * members,)),
-            dma((groups * members,)),
+            dma((devices,)),
+            dma((devices,)),
             dma((owners,)),
+            dma((devices,)),
+            dma((devices,)),
         ],
         compiler_params=pltpu.CompilerParams(
             collective_id=0, has_side_effects=True, vmem_limit_bytes=50331648

time: 31 us -> 29.8 us (0.961)
  Pallas kernels: 30.2 us -> 28.9 us
    pallas_call x1, Pallas kernels: 29.2 us -> 27.9 us  [per_device(): pl.pallas_call(functools.partial(layer_kernel, (groups, members, rows, sl...]
where the time goes in v4:
time: 29.8 us; the launch traced here: 29.6 us
  Pallas kernels  28.9 us (97%)
  between operations  0.64 us (2%)
    pallas_call x1, Pallas kernels, per_device(): pl.pallas_call(functools.partial(layer_kernel, (groups, members, rows, sl...  27.9 us
    pallas_call x1, Pallas kernels, per_device(): pl.pallas_call(push_kernel, out_shape=(jax.ShapeDtypeStruct(blocked, BF16...  1.01 us

profile of v4, /device:TPU:0, one launch (start us, length us, event | category | flops | bytes accessed | tf_op | source)
XLA Modules:
  0.0 29.6 jit_solution(16280233808124773087)
XLA Ops:
  0.6 27.9 %gcn_layer.1 = (bf16[16,128,128]{2,1,0:T(8,128)(2,1)S(1)}, bf16[16,128,128]{2,1,0:T(8,128)(2,1)S(1)}, f32[128,128]{1,0:T(8,128)S(1)}, f32[1,128]{1,0:T(1,128)S(1)}) custom-call(s32[1,1,8,16]{3,2,1,0:T(8,128)} %bitcast.15, s32[1,1,16]{2,1,0:T(1,128)} %counts.1, s32[1,1,1,8]{3,2,1,0:T(1,128)} %bitcast.17, s32[1,1,2,4]{3,2,1,0:T(2,128)} %bitcast.16, ...), custom_call_target="tpu_custom_call" | custom-call | tf_op jit(solution)/shard_map/gcn_layer/pallas_call | solution.py:432
  28.6 1.0 %push.1 = (bf16[16,128,128]{2,1,0:T(8,128)(2,1)}, bf16[16,128,128]{2,1,0:T(8,128)(2,1)}, f32[128,128]{1,0:T(8,128)}, f32[1,128]{1,0:T(1,128)}) custom-call(bf16[16,128,128]{2,1,0:T(8,128)(2,1)S(1)} %get-tuple-element.12.out, bf16[16,128,128]{2,1,0:T(8,128)(2,1)S(1)} %get-tuple-element.13.grad, f32[128,128]{1,0:T(8,128)S(1)} %get-tuple-element.14.w_sum, ...), custom_call_target="tpu_custom_call" | custom-call | tf_op jit(solution)/shard_map/push/pallas_call | solution.py:496

commit v5 on v4

--- a/solution.py
+++ b/solution.py
@@ -23,20 +23,26 @@
 
 def layer_kernel(
     dims,
+    tile_source_hbm,
+    counts_hbm,
+    requests_hbm,
+    send_ids_hbm,
+    x_hbm,
+    hist_hbm,
+    adj_hbm,
+    cot_hbm,
+    weight_hbm,
+    bias_hbm,
+    out_ref,
+    grad_ref,
+    wsum_ref,
+    bsum_ref,
     tile_source,
     counts,
     requests,
     send_ids,
-    x_hbm,
-    hist_hbm,
-    adj_hbm,
-    cot_hbm,
     weight,
     bias,
-    out_ref,
-    grad_ref,
-    wsum_ref,
-    bsum_ref,
     table,
     hist,
     adj,
@@ -98,16 +104,27 @@
     adj_copy = pltpu.make_async_copy(adj_hbm, adj, local_sem.at[1])
     x_copy = pltpu.make_async_copy(x_hbm, table.at[pl.ds(0, rows)], local_sem.at[2])
     cot_copy = pltpu.make_async_copy(cot_hbm, cot, local_sem.at[3])
-    hist_copy.start()
+    requests_copy = pltpu.make_async_copy(requests_hbm, requests, local_sem.at[5])
+    send_ids_copy = pltpu.make_async_copy(send_ids_hbm, send_ids, local_sem.at[6])
+    small = ((tile_source_hbm, tile_source), (counts_hbm, counts), (weight_hbm, weight), (bias_hbm, bias))
+    small_copies = [
+        pltpu.make_async_copy(a, b, local_sem.at[7 + i]) for i, (a, b) in enumerate(small)
+    ]
+    requests_copy.start()
     barrier = pltpu.get_barrier_semaphore()
     for step in range(1, members):
         pl.semaphore_signal(barrier, inc=1, device_id={"mem": mem_peer(step)}, device_id_type=MESH)
     for step in range(1, groups):
         pl.semaphore_signal(barrier, inc=1, device_id={"grp": grp_peer(step)}, device_id_type=MESH)
+    send_ids_copy.start()
+    hist_copy.start()
+    for copy in small_copies:
+        copy.start()
     x_copy.start()
     adj_copy.start()
     cot_copy.start()
 
+    requests_copy.wait()
     for m in range(members):
         outbox[m] = jnp.full(outbox.shape[1:], requests[0, 0, 0, m], jnp.int32)
     table[zero_block] = jnp.zeros((block, feats), BF16)
@@ -146,6 +163,7 @@
     for step in range(1, members):
         req_copy(m_me, near_peer(members - step)).start()
     hist_copy.wait()
+    send_ids_copy.wait()
     for g in range(groups):
         for b in range(per_group):
             outgoing[g, b] = hist[send_ids[0, 0, b, g]]
@@ -163,6 +181,8 @@
         served[peer] = hist[wanted]
         fetch_copy(m_me, peer).start()
 
+    for copy in small_copies:
+        copy.wait()
     lane = lax.broadcasted_iota(jnp.int32, (1, tiles), 1)
 
     def key_row(r, keys):
@@ -426,7 +446,6 @@
     sources = rows + members + groups * per_group + 1
     blocked = (rows, block, feats)
     dma = pltpu.SemaphoreType.DMA
-    smem = pl.BlockSpec(memory_space=pltpu.SMEM)
     vmem = pl.BlockSpec(memory_space=pltpu.VMEM)
     hbm = pl.BlockSpec(memory_space=pltpu.HBM)
     out, grad, w_sum, b_sum = pl.pallas_call(
@@ -437,9 +456,15 @@
             pltpu.VMEM((feats, feats), F32),
             pltpu.VMEM((1, feats), F32),
         ),
-        in_specs=[smem] * 4 + [hbm] * 4 + [vmem] * 2,
+        in_specs=[hbm] * 10,
         out_specs=(vmem,) * 4,
         scratch_shapes=[
+            pltpu.SMEM((1, 1, slots, rows), jnp.int32),
+            pltpu.SMEM(counts.shape, jnp.int32),
+            pltpu.SMEM((1, 1, 1, members), jnp.int32),
+            pltpu.SMEM((1, 1, per_group, groups), jnp.int32),
+            pltpu.VMEM(weight.shape, BF16),
+            pltpu.VMEM((1, feats), F32),
             pltpu.VMEM((sources, block, feats), BF16),
             pltpu.VMEM(blocked, BF16),
             pltpu.VMEM((rows, slots, block, block), BF16),
@@ -458,7 +483,7 @@
             pltpu.VMEM((owners, padded, feats), BF16),
             pltpu.VMEM((1, feats), F32),
             pltpu.VMEM((devices, 1, feats), F32),
-            dma((5,)),
+            dma((11,)),
             dma((members,)),
             dma((members,)),
             dma((members,)),

time: 29.8 us -> 29 us (0.973)
  Pallas kernels: 28.9 us -> 28.2 us
    pallas_call x1, Pallas kernels: 27.9 us -> 27.2 us  [per_device(): pl.pallas_call(functools.partial(layer_kernel, (groups, members, rows, sl...]
where the time goes in v5:
time: 29 us; the launch traced here: 28.9 us
  Pallas kernels  28.2 us (97%)
  between operations  0.64 us (2%)
    pallas_call x1, Pallas kernels, per_device(): pl.pallas_call(functools.partial(layer_kernel, (groups, members, rows, sl...  27.2 us
    pallas_call x1, Pallas kernels, per_device(): pl.pallas_call(push_kernel, out_shape=(jax.ShapeDtypeStruct(blocked, BF16...  1.01 us

profile of v5, /device:TPU:0, one launch (start us, length us, event | category | flops | bytes accessed | tf_op | source)
XLA Modules:
  0.0 28.9 jit_solution(6489834239381870299)
XLA Ops:
  0.6 27.2 %gcn_layer.1 = (bf16[16,128,128]{2,1,0:T(8,128)(2,1)S(1)}, bf16[16,128,128]{2,1,0:T(8,128)(2,1)S(1)}, f32[128,128]{1,0:T(8,128)S(1)}, f32[1,128]{1,0:T(1,128)S(1)}) custom-call(s32[1,1,8,16]{3,2,1,0:T(8,128)} %bitcast.15, s32[1,1,16]{2,1,0:T(1,128)} %counts_hbm.1, s32[1,1,1,8]{3,2,1,0:T(1,128)} %bitcast.17, s32[1,1,2,4]{3,2,1,0:T(2,128)} %bitcast.16, ...), custom_call_target="tpu_custom_call" | custom-call | tf_op jit(solution)/shard_map/gcn_layer/pallas_call | solution.py:451
  27.8 1.0 %push.1 = (bf16[16,128,128]{2,1,0:T(8,128)(2,1)}, bf16[16,128,128]{2,1,0:T(8,128)(2,1)}, f32[128,128]{1,0:T(8,128)}, f32[1,128]{1,0:T(1,128)}) custom-call(bf16[16,128,128]{2,1,0:T(8,128)(2,1)S(1)} %get-tuple-element.12.out, bf16[16,128,128]{2,1,0:T(8,128)(2,1)S(1)} %get-tuple-element.13.grad, f32[128,128]{1,0:T(8,128)S(1)} %get-tuple-element.14.w_sum, ...), custom_call_target="tpu_custom_call" | custom-call | tf_op jit(solution)/shard_map/push/pallas_call | solution.py:521

commit v6 on v5

--- a/solution.py
+++ b/solution.py
@@ -14,6 +14,7 @@
 GELU_C = math.sqrt(2.0 / math.pi)
 GELU_A = 0.044715
 PAIR_UNROLL = 24
+EARLY_UNROLL = 8
 CHUNK_ROWS = 4
 
 
@@ -51,6 +52,9 @@
     inbox,
     served,
     outgoing,
+    late,
+    combined,
+    partial,
     grad_pre,
     grad_t,
     running,
@@ -75,7 +79,7 @@
     bias_send,
     bias_recv,
 ):
-    groups, members, rows, slots, per_group, scale, first_owner, span, stride = dims
+    groups, members, rows, slots, per_group, scale, first_owner, span, stride, split = dims
     tiles = rows * slots
     owners = groups // stride * span
     share = weight.shape[0] // owners
@@ -85,6 +89,7 @@
     feats = hist.shape[2]
     zero_block = table.shape[0] - 1
     border_at = rows + members
+    half = members // 2
 
     def mem_peer(step):
         return lax.rem(m_me + step, members)
@@ -150,6 +155,16 @@
             device_id_type=MESH,
         )
 
+    def late_copy(slot_there, peer):
+        return pltpu.make_async_remote_copy(
+            src_ref=served.at[peer],
+            dst_ref=late.at[lax.rem(slot_there, half)],
+            send_sem=fetch_send.at[peer],
+            recv_sem=fetch_recv.at[slot_there],
+            device_id={"mem": peer},
+            device_id_type=MESH,
+        )
+
     def border_copy(slot_there, peer):
         return pltpu.make_async_remote_copy(
             src_ref=outgoing.at[peer],
@@ -179,7 +194,18 @@
         req_copy(peer, peer).wait_recv()
         wanted = inbox[peer][0, 0]
         served[peer] = hist[wanted]
-        fetch_copy(m_me, peer).start()
+        if split:
+            beside = peer // half == m_me // half
+
+            @pl.when(beside)
+            def _():
+                fetch_copy(m_me, peer).start()
+
+            @pl.when(jnp.logical_not(beside))
+            def _():
+                late_copy(m_me, peer).start()
+        else:
+            fetch_copy(m_me, peer).start()
 
     for copy in small_copies:
         copy.wait()
@@ -227,26 +253,58 @@
     running[0] = jnp.zeros((feats, block), F32)
     grad_t[0] = jnp.zeros((feats, block), BF16)
 
+    late_base = half - m_me // half * half if split else members
+    late_at = rows + late_base
+
+    def gather_row(r):
+        live = counts[0, 0, r]
+        sources = []
+        for k in range(slots):
+            source = tile_source[0, 0, k, r]
+            early = (source < late_at) | (source >= late_at + half) if split else True
+            sources.append(table[jnp.where((k < live) & early, source, zero_block)])
+        wide = jnp.concatenate([adj[r, k] for k in range(slots)], axis=1)
+        tall = jnp.concatenate(sources, axis=0)
+        return dot(wide, tall, ((1,), (0,)))
+
+    def combine_row(r, carry):
+        live = counts[0, 0, r]
+        sums = [jnp.zeros((block, block), BF16)] * half
+        for k in range(slots):
+            source = jnp.where(k < live, tile_source[0, 0, k, r], zero_block)
+            tile = adj[r, k]
+            for s in range(half):
+                sums[s] = sums[s] + jnp.where(source == late_at + s, tile, jnp.zeros_like(tile))
+        for s in range(half):
+            combined[r, :, s * block : (s + 1) * block] = sums[s]
+        return carry
+
+    def early_rows(i, carry):
+        for u in range(EARLY_UNROLL):
+            r = i * EARLY_UNROLL + u
+            partial[r] = gather_row(r)
+        return carry
+
     x_copy.wait()
     adj_copy.wait()
     cot_copy.wait()
+    if split:
+        lax.fori_loop(0, rows, combine_row, jnp.int32(0))
     sort_copy.wait()
     for step in range(1, groups):
         peer = grp_peer(step)
         border_copy(peer, peer).wait_recv()
-    for step in range(1, members):
-        peer = mem_peer(step)
-        fetch_copy(peer, peer).wait_recv()
-
-    def gather_row(r):
-        live = counts[0, 0, r]
-        sources = []
-        for k in range(slots):
-            at = jnp.where(k < live, tile_source[0, 0, k, r], zero_block)
-            sources.append(table[at])
-        wide = jnp.concatenate([adj[r, k] for k in range(slots)], axis=1)
-        tall = jnp.concatenate(sources, axis=0)
-        return dot(wide, tall, ((1,), (0,))).astype(BF16)
+    if split:
+        for step in range(1, half):
+            peer = half - late_base + lax.rem(lax.rem(m_me, half) + step, half)
+            fetch_copy(peer, peer).wait_recv()
+        lax.fori_loop(0, rows // EARLY_UNROLL, early_rows, jnp.int32(0))
+        for step in range(half):
+            late_copy(late_base + step, late_base + step).wait_recv()
+    else:
+        for step in range(1, members):
+            peer = mem_peer(step)
+            fetch_copy(peer, peer).wait_recv()
 
     nodes = CHUNK_ROWS * block
 
@@ -265,7 +323,15 @@
         return w_part, jnp.sum(grads.astype(F32), axis=0, keepdims=True)
 
     def gather_chunk(i):
-        return jnp.concatenate([gather_row(i * CHUNK_ROWS + u) for u in range(CHUNK_ROWS)], axis=0)
+        if split:
+            part = pl.ds(i * CHUNK_ROWS, CHUNK_ROWS)
+            wide = combined[part].reshape(nodes, half * block)
+            tall = late[...].reshape(half * block, feats)
+            agg = partial[part].reshape(nodes, feats) + dot(wide, tall, ((1,), (0,)))
+        else:
+            at = range(i * CHUNK_ROWS, (i + 1) * CHUNK_ROWS)
+            agg = jnp.concatenate([gather_row(r) for r in at], axis=0)
+        return agg.astype(BF16)
 
     w_sum = jnp.zeros((feats, feats), F32)
     b_sum = jnp.zeros((1, feats), F32)
@@ -434,7 +500,8 @@
     per_group = send_ids.shape[3]
     assert requests.shape[3] == 1
     tiles = rows * slots
-    assert rows % CHUNK_ROWS == 0 and (tiles + rows) % (2 * PAIR_UNROLL) == 0
+    split = members % 2 == 0 and members // 2 < slots
+    assert rows % CHUNK_ROWS == 0 and rows % EARLY_UNROLL == 0 and (tiles + rows) % (2 * PAIR_UNROLL) == 0
     scale = (layer_input.shape[0] * groups * members) ** (-0.5)
     stride = 2 if groups % 2 == 0 else 1
     columns = groups // stride
@@ -449,7 +516,7 @@
     vmem = pl.BlockSpec(memory_space=pltpu.VMEM)
     hbm = pl.BlockSpec(memory_space=pltpu.HBM)
     out, grad, w_sum, b_sum = pl.pallas_call(
-        functools.partial(layer_kernel, (groups, members, rows, slots, per_group, scale, first_owner, span, stride)),
+        functools.partial(layer_kernel, (groups, members, rows, slots, per_group, scale, first_owner, span, stride, split)),
         out_shape=(
             pltpu.VMEM(blocked, BF16),
             pltpu.VMEM(blocked, BF16),
@@ -473,6 +540,9 @@
             pltpu.VMEM((members, 1, 128), jnp.int32),
             pltpu.VMEM((members, block, feats), BF16),
             pltpu.VMEM((groups, per_group, block, feats), BF16),
+            pltpu.VMEM((members // 2, block, feats) if split else (8, 128), BF16),
+            pltpu.VMEM((rows, block, members // 2 * block) if split else (8, 128), BF16),
+            pltpu.VMEM((rows, block, feats) if split else (8, 128), F32),
             pltpu.VMEM(blocked, BF16),
             pltpu.VMEM((rows + 1, feats, block), BF16),
             pltpu.VMEM(((tiles + rows) // 2 + 1, feats, block), F32),

time: 29 us -> 28.4 us (0.979)
  Pallas kernels: 28.2 us -> 27.6 us
    pallas_call x1, Pallas kernels: 27.2 us -> 26.6 us  [per_device(): pl.pallas_call(functools.partial(layer_kernel, (groups, members, rows, sl...]
where the time goes in v6:
time: 28.4 us; the launch traced here: 28.3 us
  Pallas kernels  27.6 us (97%)
  between operations  0.64 us (2%)
    pallas_call x1, Pallas kernels, per_device(): pl.pallas_call(functools.partial(layer_kernel, (groups, members, rows, sl...  26.6 us
    pallas_call x1, Pallas kernels, per_device(): pl.pallas_call(push_kernel, out_shape=(jax.ShapeDtypeStruct(blocked, BF16...  1.01 us

profile of v6, /device:TPU:0, one launch (start us, length us, event | category | flops | bytes accessed | tf_op | source)
XLA Modules:
  0.0 28.3 jit_solution(9668471168572141093)
XLA Ops:
  0.6 26.6 %gcn_layer.1 = (bf16[16,128,128]{2,1,0:T(8,128)(2,1)S(1)}, bf16[16,128,128]{2,1,0:T(8,128)(2,1)S(1)}, f32[128,128]{1,0:T(8,128)S(1)}, f32[1,128]{1,0:T(1,128)S(1)}) custom-call(s32[1,1,8,16]{3,2,1,0:T(8,128)} %bitcast.15, s32[1,1,16]{2,1,0:T(1,128)} %counts_hbm.1, s32[1,1,1,8]{3,2,1,0:T(1,128)} %bitcast.17, s32[1,1,2,4]{3,2,1,0:T(2,128)} %bitcast.16, ...), custom_call_target="tpu_custom_call" | custom-call | tf_op jit(solution)/shard_map/gcn_layer/pallas_call | solution.py:518
  27.3 1.0 %push.1 = (bf16[16,128,128]{2,1,0:T(8,128)(2,1)}, bf16[16,128,128]{2,1,0:T(8,128)(2,1)}, f32[128,128]{1,0:T(8,128)}, f32[1,128]{1,0:T(1,128)}) custom-call(bf16[16,128,128]{2,1,0:T(8,128)(2,1)S(1)} %get-tuple-element.12.out, bf16[16,128,128]{2,1,0:T(8,128)(2,1)S(1)} %get-tuple-element.13.grad, f32[128,128]{1,0:T(8,128)S(1)} %get-tuple-element.14.w_sum, ...), custom_call_target="tpu_custom_call" | custom-call | tf_op jit(solution)/shard_map/push/pallas_call | solution.py:591

commit v7 on v6

--- a/solution.py
+++ b/solution.py
@@ -16,6 +16,7 @@
 PAIR_UNROLL = 24
 EARLY_UNROLL = 8
 CHUNK_ROWS = 4
+CHUNKS = (2,)
 
 
 def dot(a, b, contract):
@@ -55,6 +56,7 @@
     late,
     combined,
     partial,
+    agg_all,
     grad_pre,
     grad_t,
     running,
@@ -306,43 +308,45 @@
             peer = mem_peer(step)
             fetch_copy(peer, peer).wait_recv()
 
-    nodes = CHUNK_ROWS * block
-
-    def activate(r, agg):
+    def activate(r, count, agg):
+        nodes = count * block
         pre = dot(agg, weight[...], ((1,), (0,))) + bias[...]
         square = pre * pre
         t = jnp.tanh(pre * (GELU_C + (GELU_C * GELU_A) * square))
-        half = 0.5 + 0.5 * t
-        out_ref[pl.ds(r, CHUNK_ROWS)] = (pre * half).astype(BF16).reshape(CHUNK_ROWS, block, feats)
+        half_up = 0.5 + 0.5 * t
+        out_ref[pl.ds(r, count)] = (pre * half_up).astype(BF16).reshape(count, block, feats)
         rise = 2.0 * GELU_C + (6.0 * GELU_C * GELU_A) * square
-        slope = half + half * (((1.0 - half) * pre) * rise)
-        cots = cot[pl.ds(r, CHUNK_ROWS)].reshape(nodes, feats).astype(F32)
+        slope = half_up + half_up * (((1.0 - half_up) * pre) * rise)
+        cots = cot[pl.ds(r, count)].reshape(nodes, feats).astype(F32)
         grads = (cots * slope).astype(BF16)
-        grad_pre[pl.ds(r, CHUNK_ROWS)] = grads.reshape(CHUNK_ROWS, block, feats)
-        w_part = dot(agg, grads, ((0,), (0,)))
-        return w_part, jnp.sum(grads.astype(F32), axis=0, keepdims=True)
-
-    def gather_chunk(i):
+        agg_all[pl.ds(r, count)] = agg.reshape(count, block, feats)
+        grad_pre[pl.ds(r, count)] = grads.reshape(count, block, feats)
+        return None, jnp.sum(grads.astype(F32), axis=0, keepdims=True)
+
+    def gather_chunk(r, count):
         if split:
-            part = pl.ds(i * CHUNK_ROWS, CHUNK_ROWS)
+            part = pl.ds(r, count)
+            nodes = count * block
             wide = combined[part].reshape(nodes, half * block)
             tall = late[...].reshape(half * block, feats)
             agg = partial[part].reshape(nodes, feats) + dot(wide, tall, ((1,), (0,)))
         else:
-            at = range(i * CHUNK_ROWS, (i + 1) * CHUNK_ROWS)
-            agg = jnp.concatenate([gather_row(r) for r in at], axis=0)
+            agg = jnp.concatenate([gather_row(r + u) for u in range(count)], axis=0)
         return agg.astype(BF16)
 
-    w_sum = jnp.zeros((feats, feats), F32)
     b_sum = jnp.zeros((1, feats), F32)
-    chunks = rows // CHUNK_ROWS
-    held = gather_chunk(0)
-    for i in range(chunks):
-        following = gather_chunk(i + 1) if i + 1 < chunks else None
-        w_part, b_part = activate(i * CHUNK_ROWS, held)
-        w_sum = w_sum + w_part
+    starts = []
+    while not starts or sum(starts[-1]) < rows:
+        at = sum(starts[-1]) if starts else 0
+        starts.append((at, min(CHUNKS[min(len(starts), len(CHUNKS) - 1)], rows - at)))
+    held = gather_chunk(*starts[0])
+    for i, (r, count) in enumerate(starts):
+        following = gather_chunk(*starts[i + 1]) if i + 1 < len(starts) else None
+        _, b_part = activate(r, count, held)
         b_sum = b_sum + b_part
         held = following
+    whole = (rows * block, feats)
+    w_sum = dot(agg_all[...].reshape(whole), grad_pre[...].reshape(whole), ((0,), (0,)))
 
     padding = jnp.zeros((parts.shape[1] - share, feats), F32)
     for o in range(owners):
@@ -354,6 +358,11 @@
     devices = groups * members
     owning = (lax.rem(g_me, stride) == stride - 1) & (m_me >= first_owner) & (m_me < first_owner + span)
     own = g_me // stride * span + jnp.clip(m_me - first_owner, 0, span - 1)
+
+    ends_first = sorted(range(members), key=lambda m: -abs(2 * m - members + 1))
+    far_groups = list(range(1, groups, 2)) + list(range(2, groups, 2))
+    others = [grp_peer(step) * members + m for step in far_groups for m in ends_first]
+    others += [g_me * members + mem_peer(step) for step in range(1, members)]
 
     def a_copy(owner, sender):
         return pltpu.make_async_remote_copy(
@@ -399,6 +408,7 @@
     for step in range(1, devices):
         bias_copy(me, lax.rem(me + step, devices)).start()
 
+    nodes = CHUNK_ROWS * block
     for i in range(rows // CHUNK_ROWS):
         grads = grad_pre[pl.ds(i * CHUNK_ROWS, CHUNK_ROWS)].reshape(nodes, feats)
         flipped = dot(weight[...], grads, ((1,), (1,))).astype(BF16)
@@ -427,15 +437,13 @@
 
     @pl.when(owning)
     def _():
-        scattered[me] = parts[own]
-        for step in range(1, devices):
-            a_copy(own, lax.rem(me + step, devices)).wait_recv()
-        chunk = scattered[0].astype(F32)
-        for d in range(1, devices):
-            chunk = chunk + scattered[d].astype(F32)
+        chunk = parts[own].astype(F32)
+        for device in reversed(others):
+            a_copy(own, device).wait_recv()
+            chunk = chunk + scattered[device].astype(F32)
         result[own] = (chunk * scale).astype(BF16)
-        for step in range(1, devices):
-            b_copy(own, lax.rem(me + step, devices)).start()
+        for device in others:
+            b_copy(own, device).start()
 
     for step in range(1, members):
         peer = mem_peer(step)
@@ -544,6 +552,7 @@
             pltpu.VMEM((rows, block, members // 2 * block) if split else (8, 128), BF16),
             pltpu.VMEM((rows, block, feats) if split else (8, 128), F32),
             pltpu.VMEM(blocked, BF16),
+            pltpu.VMEM(blocked, BF16),
             pltpu.VMEM((rows + 1, feats, block), BF16),
             pltpu.VMEM(((tiles + rows) // 2 + 1, feats, block), F32),
             pltpu.VMEM((8, tiles), jnp.int32),

time: 28.4 us -> 28 us (0.986)
  Pallas kernels: 27.6 us -> 27.2 us
    pallas_call x1, Pallas kernels: 26.6 us -> 26.2 us  [per_device(): pl.pallas_call(functools.partial(layer_kernel, (groups, members, rows, sl...]
where the time goes in v7:
time: 28 us; the launch traced here: 27.9 us
  Pallas kernels  27.2 us (97%)
  between operations  0.64 us (2%)
    pallas_call x1, Pallas kernels, per_device(): pl.pallas_call(functools.partial(layer_kernel, (groups, members, rows, sl...  26.2 us
    pallas_call x1, Pallas kernels, per_device(): pl.pallas_call(push_kernel, out_shape=(jax.ShapeDtypeStruct(blocked, BF16...  1.01 us

profile of v7, /device:TPU:0, one launch (start us, length us, event | category | flops | bytes accessed | tf_op | source)
XLA Modules:
  0.0 27.9 jit_solution(17124080956645437891)
XLA Ops:
  0.6 26.2 %gcn_layer.1 = (bf16[16,128,128]{2,1,0:T(8,128)(2,1)S(1)}, bf16[16,128,128]{2,1,0:T(8,128)(2,1)S(1)}, f32[128,128]{1,0:T(8,128)S(1)}, f32[1,128]{1,0:T(1,128)S(1)}) custom-call(s32[1,1,8,16]{3,2,1,0:T(8,128)} %bitcast.15, s32[1,1,16]{2,1,0:T(1,128)} %counts_hbm.1, s32[1,1,1,8]{3,2,1,0:T(1,128)} %bitcast.17, s32[1,1,2,4]{3,2,1,0:T(2,128)} %bitcast.16, ...), custom_call_target="tpu_custom_call" | custom-call | tf_op jit(solution)/shard_map/gcn_layer/pallas_call | solution.py:526
  26.9 1.0 %push.1 = (bf16[16,128,128]{2,1,0:T(8,128)(2,1)}, bf16[16,128,128]{2,1,0:T(8,128)(2,1)}, f32[128,128]{1,0:T(8,128)}, f32[1,128]{1,0:T(1,128)}) custom-call(bf16[16,128,128]{2,1,0:T(8,128)(2,1)S(1)} %get-tuple-element.12.out, bf16[16,128,128]{2,1,0:T(8,128)(2,1)S(1)} %get-tuple-element.13.grad, f32[128,128]{1,0:T(8,128)S(1)} %get-tuple-element.14.w_sum, ...), custom_call_target="tpu_custom_call" | custom-call | tf_op jit(solution)/shard_map/push/pallas_call | solution.py:600
